TPU v7x, 16 devices: a 4x2x1 block of a 4x4x8 slice. The times are simulated.
16 devices in a mesh: prob: 2 (over y, z), feat: 8 (over x, core).
Axes of the slice: x: 4, y: 2, z: 1, core: 2. Of those that a mesh axis runs over, the one named last changes fastest.
The devices are a block of a 4x4x8 slice.
Arguments:
- design: bfloat16 [32768, 16384], P('prob', 'feat'), parts along dimension 0
- targets: float32 [32768, 200], P('prob'), parts along dimension 0
- weights_init: float32 [32768, 200], P(('prob', 'feat')), parts along dimension 0
- step_sizes: float32 [32768], P(('prob', 'feat')), parts along dimension 0
Outputs:
- output 1: float32 [32768, 200], P(('prob', 'feat')), parts along dimension 0
- output 2: float32 [32768, 200], P('prob'), parts along dimension 0
There are 2 independent parts. A program takes and returns all parts, laid end to end along the dimension named above; each array names one.
All inputs are finite; a program needn't handle non-finite values.
Results may differ from a plain program's by a relative error of at most 0.001.
Values are sent between devices in bfloat16 or wider.
A program may use at most 768 MiB of HBM per device.

v0:
```python
import jax
import jax.numpy as jnp
from jax import lax
from jax.sharding import PartitionSpec as P, NamedSharding

SWEEPS = 6
RIDGE_COEF = 1.0
MIX_WEIGHT = 0.75


def solution(mesh):
    def local_solve(design, targets, weights, step_sizes):
        samples = design.shape[0]
        ridge_val = RIDGE_COEF / samples
        step_col = step_sizes[:, None]
        partial = jnp.dot(design, weights.astype(jnp.bfloat16), preferred_element_type=jnp.float32)
        residual = targets - lax.psum(partial, 'feat')
        for _ in range(SWEEPS):
            gradient = lax.dot_general(design, residual.astype(jnp.bfloat16), (((0,), (0,)), ((), ())), preferred_element_type=jnp.float32) / samples
            update = step_col * (gradient - ridge_val * weights)
            weights = weights + MIX_WEIGHT * update
            contrib = jnp.dot(design, update.astype(jnp.bfloat16), preferred_element_type=jnp.float32)
            residual = residual - MIX_WEIGHT * lax.psum(contrib, 'feat')
        return weights, residual

    return jax.shard_map(
        local_solve,
        mesh=mesh,
        in_specs=(P('prob', 'feat'), P('prob', None), P(('prob', 'feat'), None), P(('prob', 'feat'))),
        out_specs=(P(('prob', 'feat'), None), P('prob', None)),
        check_vma=False,
    )
```

profile of v0, /device:TPU:113, one launch (start us, length us, event | category | flops | bytes accessed | tf_op | source)
XLA Modules:
  0.0 1484.3 jit_solution(4013784334765975742)
XLA Ops:
  7.2 34.7 %fusion.90 = f32[16384,200]{0,1:T(8,128)} fusion(bf16[16384,2048]{1,0:T(8,128)(2,1)} %param.4, f32[2048,200]{0,1:T(8,128)} %param.6), kind=kOutput, calls=%fused_computation.60 | convolution fusion | flops 13422182400 | bytes 81854464 | tf_op jit(solution)/shard_map/dot_general | solution.py:16
  42.1 143.3 %all-reduce.8.cloned.1.call-done = f32[16384,200]{0,1:T(8,128)} async-done(((f32[16384,200]{0,1:T(8,128)}), f32[16384,200]{0,1:T(8,128)}) %all-reduce.8.cloned.1.call-update) | async-done | bytes 13107216 | tf_op jit(solution)/shard_map/psum | solution.py:17
  185.4 14.4 sub.39
  199.8 27.7 %fusion.69 = f32[2048,200]{0,1:T(8,128)S(1)} fusion(bf16[16384,2048]{1,0:T(8,128)(2,1)} %param.4, f32[16384,200]{0,1:T(8,128)} %sub.39, f32[2048,200]{0,1:T(8,128)S(1)} %copy-done, f32[2048]{0:T(1024)S(1)} %copy-done.1), kind=kOutput, calls=%fused_computation.43 | convolution fusion | flops 13426688000 | bytes 83501056 | tf_op jit(solution)/shard_map/dot_general | solution.py:19
  227.5 33.4 %convolution_bitcast_fusion.5 = f32[16384,200]{0,1:T(8,128)} fusion(bf16[16384,2048]{1,0:T(8,128)(2,1)} %param.4, f32[2048,200]{0,1:T(8,128)S(1)} %fusion.69), kind=kOutput, calls=%fused_computation.5 | convolution fusion | flops 13422182400 | bytes 81854464 | tf_op jit(solution)/shard_map/dot_general | solution.py:22
  261.5 139.9 %all-reduce.10.cloned.1.call-done = f32[16384,200]{0,1:T(8,128)} async-done(((f32[16384,200]{0,1:T(8,128)}), f32[16384,200]{0,1:T(8,128)}) %all-reduce.10.cloned.1.call-update) | async-done | bytes 13107216 | tf_op jit(solution)/shard_map/psum | solution.py:23
  401.4 33.3 %multiply_add_fusion.4 = (f32[2048,200]{0,1:T(8,128)S(1)}, bf16[2048,200]{0,1:T(8,128)(2,1)}) fusion(f32[2048,200]{0,1:T(8,128)S(1)} %copy-done, f32[2048,200]{0,1:T(8,128)} %copy-done.3, bf16[16384,2048]{1,0:T(8,128)(2,1)} %param.4, f32[16384,200]{0,1:T(8,128)} %sub.39, f32[16384,200]{0,1:T(8,128)} %all-reduce.10.cloned.1.call-done, f32[2048]{0:T(1024)S(1)} %copy-done.1), kind=kOutput, calls=%fused_computation.52 | convolution fusion | flops 13435289600 | bytes 99065856 | tf_op jit(solution)/shard_map/dot_general | solution.py:19
  434.8 32.2 %convolution_bitcast_fusion.4 = f32[16384,200]{0,1:T(8,128)} fusion(bf16[16384,2048]{1,0:T(8,128)(2,1)} %param.4, bf16[2048,200]{0,1:T(8,128)(2,1)} %get-tuple-element.3), kind=kOutput, calls=%fused_computation.4 | convolution fusion | flops 13421772800 | bytes 81035264 | tf_op jit(solution)/shard_map/dot_general | solution.py:22
  467.3 140.3 %all-reduce.12.cloned.1.call-done = f32[16384,200]{0,1:T(8,128)} async-done(((f32[16384,200]{0,1:T(8,128)}), f32[16384,200]{0,1:T(8,128)}) %all-reduce.12.cloned.1.call-update) | async-done | bytes 13107216 | tf_op jit(solution)/shard_map/psum | solution.py:23
  607.5 18.2 %multiply_subtract_fusion.4 = f32[16384,200]{0,1:T(8,128)} fusion(f32[16384,200]{0,1:T(8,128)} %all-reduce.12.cloned.1.call-done, f32[16384,200]{0,1:T(8,128)} %sub.39, f32[16384,200]{0,1:T(8,128)} %all-reduce.10.cloned.1.call-done), kind=kLoop, calls=%fused_computation.10 | loop fusion | flops 13107200 | bytes 52428800 | tf_op jit(solution)/shard_map/sub | solution.py:23
  625.7 27.7 %fusion.75 = f32[2048,200]{0,1:T(8,128)S(1)} fusion(bf16[16384,2048]{1,0:T(8,128)(2,1)} %param.4, f32[16384,200]{0,1:T(8,128)} %multiply_subtract_fusion.4, f32[2048,200]{0,1:T(8,128)S(1)} %get-tuple-element.2, f32[2048]{0:T(1024)S(1)} %copy-done.1), kind=kOutput, calls=%fused_computation.45 | convolution fusion | flops 13426688000 | bytes 83501056 | tf_op jit(solution)/shard_map/dot_general | solution.py:19
  653.4 33.3 %convolution_bitcast_fusion.3 = f32[16384,200]{0,1:T(8,128)} fusion(bf16[16384,2048]{1,0:T(8,128)(2,1)} %param.4, f32[2048,200]{0,1:T(8,128)S(1)} %fusion.75), kind=kOutput, calls=%fused_computation.3 | convolution fusion | flops 13422182400 | bytes 81854464 | tf_op jit(solution)/shard_map/dot_general | solution.py:22
  687.1 140.2 %all-reduce.14.cloned.1.call-done = f32[16384,200]{0,1:T(8,128)} async-done(((f32[16384,200]{0,1:T(8,128)}), f32[16384,200]{0,1:T(8,128)}) %all-reduce.14.cloned.1.call-update) | async-done | bytes 13107216 | tf_op jit(solution)/shard_map/psum | solution.py:23
  827.3 33.3 %multiply_add_fusion.2 = (f32[2048,200]{0,1:T(8,128)S(1)}, bf16[2048,200]{0,1:T(8,128)(2,1)}) fusion(f32[2048,200]{0,1:T(8,128)S(1)} %get-tuple-element.2, f32[2048,200]{0,1:T(8,128)} %copy-done.2, bf16[16384,2048]{1,0:T(8,128)(2,1)} %param.4, f32[16384,200]{0,1:T(8,128)} %multiply_subtract_fusion.4, f32[16384,200]{0,1:T(8,128)} %all-reduce.14.cloned.1.call-done, ...), kind=kOutput, calls=%fused_computation.50 | convolution fusion | flops 13435289600 | bytes 99065856 | tf_op jit(solution)/shard_map/dot_general | solution.py:19
  860.6 32.2 %convolution_bitcast_fusion.2 = f32[16384,200]{0,1:T(8,128)} fusion(bf16[16384,2048]{1,0:T(8,128)(2,1)} %param.4, bf16[2048,200]{0,1:T(8,128)(2,1)} %get-tuple-element.5), kind=kOutput, calls=%fused_computation.2 | convolution fusion | flops 13421772800 | bytes 81035264 | tf_op jit(solution)/shard_map/dot_general | solution.py:22
  893.2 140.2 %all-reduce.16.cloned.1.call-done = f32[16384,200]{0,1:T(8,128)} async-done(((f32[16384,200]{0,1:T(8,128)}), f32[16384,200]{0,1:T(8,128)}) %all-reduce.16.cloned.1.call-update) | async-done | bytes 13107216 | tf_op jit(solution)/shard_map/psum | solution.py:23
  1033.3 18.2 %multiply_subtract_fusion.2 = f32[16384,200]{0,1:T(8,128)} fusion(f32[16384,200]{0,1:T(8,128)} %all-reduce.16.cloned.1.call-done, f32[16384,200]{0,1:T(8,128)} %multiply_subtract_fusion.4, f32[16384,200]{0,1:T(8,128)} %all-reduce.14.cloned.1.call-done), kind=kLoop, calls=%fused_computation.8 | loop fusion | flops 13107200 | bytes 52428800 | tf_op jit(solution)/shard_map/sub | solution.py:23
  1051.6 27.7 %fusion.81 = f32[2048,200]{0,1:T(8,128)S(1)} fusion(bf16[16384,2048]{1,0:T(8,128)(2,1)} %param.4, f32[16384,200]{0,1:T(8,128)} %multiply_subtract_fusion.2, f32[2048,200]{0,1:T(8,128)S(1)} %get-tuple-element.4, f32[2048]{0:T(1024)S(1)} %copy-done.1), kind=kOutput, calls=%fused_computation.47 | convolution fusion | flops 13426688000 | bytes 83501056 | tf_op jit(solution)/shard_map/dot_general | solution.py:19
  1079.2 32.8 %convolution_bitcast_fusion.1 = f32[16384,200]{0,1:T(8,128)} fusion(bf16[16384,2048]{1,0:T(8,128)(2,1)} %param.4, f32[2048,200]{0,1:T(8,128)S(1)} %fusion.81), kind=kOutput, calls=%fused_computation.1 | convolution fusion | flops 13422182400 | bytes 81854464 | tf_op jit(solution)/shard_map/dot_general | solution.py:22
  1112.5 140.1 %all-reduce.18.cloned.1.call-done = f32[16384,200]{0,1:T(8,128)} async-done(((f32[16384,200]{0,1:T(8,128)}), f32[16384,200]{0,1:T(8,128)}) %all-reduce.18.cloned.1.call-update) | async-done | bytes 13107216 | tf_op jit(solution)/shard_map/psum | solution.py:23
  1252.6 33.3 %multiply_add_fusion = (f32[2048,200]{0,1:T(8,128)}, bf16[2048,200]{0,1:T(8,128)(2,1)}) fusion(f32[2048,200]{0,1:T(8,128)S(1)} %get-tuple-element.4, f32[2048,200]{0,1:T(8,128)S(1)} %fusion.81, bf16[16384,2048]{1,0:T(8,128)(2,1)} %param.4, f32[16384,200]{0,1:T(8,128)} %multiply_subtract_fusion.2, f32[16384,200]{0,1:T(8,128)} %all-reduce.18.cloned.1.call-done, ...), kind=kOutput, calls=%fused_computation.48 | convolution fusion | flops 13435289600 | bytes 99065856 | tf_op jit(solution)/shard_map/dot_general | solution.py:19
  1286.0 32.2 %convolution_bitcast_fusion = f32[16384,200]{0,1:T(8,128)} fusion(bf16[16384,2048]{1,0:T(8,128)(2,1)} %param.4, bf16[2048,200]{0,1:T(8,128)(2,1)} %get-tuple-element.7), kind=kOutput, calls=%fused_computation | convolution fusion | flops 13421772800 | bytes 81035264 | tf_op jit(solution)/shard_map/dot_general | solution.py:22
  1318.2 140.5 %all-reduce.20.cloned.1.call-done = f32[16384,200]{0,1:T(8,128)} async-done(((f32[16384,200]{0,1:T(8,128)}), f32[16384,200]{0,1:T(8,128)}) %all-reduce.20.cloned.1.call-update) | async-done | bytes 13107216 | tf_op jit(solution)/shard_map/psum | solution.py:23
  1458.7 18.2 %multiply_subtract_fusion = f32[16384,200]{0,1:T(8,128)} fusion(f32[16384,200]{0,1:T(8,128)} %all-reduce.20.cloned.1.call-done, f32[16384,200]{0,1:T(8,128)} %multiply_subtract_fusion.2, f32[16384,200]{0,1:T(8,128)} %all-reduce.18.cloned.1.call-done), kind=kLoop, calls=%fused_computation.6 | loop fusion | flops 13107200 | bytes 52428800 | tf_op jit(solution)/shard_map/sub | solution.py:23
  (22 shorter events, 2.3 us)
Async XLA Ops:
  7.2 178.2 %all-reduce.8.cloned.1.call-start = ((), (), s32[]{:S(2)}) async-start(), calls=%async_computation | async-start | bytes 26214400 | tf_op jit(solution)/shard_map/psum | solution.py:17
  42.0 157.8 %copy-start = (f32[2048,200]{0,1:T(8,128)S(1)}, f32[2048,200]{0,1:T(8,128)}, u32[]{:S(2)}) copy-start(f32[2048,200]{0,1:T(8,128)} %param.6) | copy-start | bytes 4915204
  42.0 157.7 %copy-start.1 = (f32[2048]{0:T(1024)S(1)}, f32[2048]{0:T(1024)}, u32[]{:S(2)}) copy-start(f32[2048]{0:T(1024)} %param.7) | copy-start | bytes 24580
  42.0 359.4 %all-reduce.10.cloned.1.call-start = ((), (), s32[]{:S(2)}) async-start(), calls=%async_computation.1 | async-start | bytes 26214400 | tf_op jit(solution)/shard_map/psum | solution.py:23
  227.5 33.4 %copy-start.3 = (f32[2048,200]{0,1:T(8,128)}, f32[2048,200]{0,1:T(8,128)S(1)}, u32[]{:S(2)}) copy-start(f32[2048,200]{0,1:T(8,128)S(1)} %fusion.69) | copy-start | bytes 4915204
  261.0 346.6 %all-reduce.12.cloned.1.call-start = ((), (), s32[]{:S(2)}) async-start(), calls=%async_computation.2 | async-start | bytes 26214400 | tf_op jit(solution)/shard_map/psum | solution.py:23
  467.0 360.3 %all-reduce.14.cloned.1.call-start = ((), (), s32[]{:S(2)}) async-start(), calls=%async_computation.3 | async-start | bytes 26214400 | tf_op jit(solution)/shard_map/psum | solution.py:23
  653.4 33.4 %copy-start.2 = (f32[2048,200]{0,1:T(8,128)}, f32[2048,200]{0,1:T(8,128)S(1)}, u32[]{:S(2)}) copy-start(f32[2048,200]{0,1:T(8,128)S(1)} %fusion.75) | copy-start | bytes 4915204
  686.8 346.5 %all-reduce.16.cloned.1.call-start = ((), (), s32[]{:S(2)}) async-start(), calls=%async_computation.4 | async-start | bytes 26214400 | tf_op jit(solution)/shard_map/psum | solution.py:23
  892.8 359.8 %all-reduce.18.cloned.1.call-start = ((), (), s32[]{:S(2)}) async-start(), calls=%async_computation.5 | async-start | bytes 26214400 | tf_op jit(solution)/shard_map/psum | solution.py:23
  1112.1 346.6 %all-reduce.20.cloned.1.call-start = ((), (), s32[]{:S(2)}) async-start(), calls=%async_computation.6 | async-start | bytes 26214400 | tf_op jit(solution)/shard_map/psum | solution.py:23
Sparse Core Ops, SparseCore 0:
  42.1 143.1 all-reduce.7
  261.1 140.3 all-reduce.9
  467.1 140.3 all-reduce.11
  687.0 140.3 all-reduce.13
  893.0 140.3 all-reduce.15
  1112.2 140.3 all-reduce.17
  1318.3 140.3 all-reduce.19
where the time goes:
time: 1490 us; the launch traced here: 1480 us
  waiting for transfers between devices  985 us (66%)
  matrix products  414 us (28%)
  other arithmetic  69.1 us (5%)
    psum x6, waiting for transfers between devices, local_solve(): residual = residual - MIX_WEIGHT * lax.psum(contrib, 'feat')  841 us
    dot_general x6, matrix products, local_solve(): jnp.dot(design, update.astype(jnp.bfloat16), preferred_element_type=jnp.f...  196 us
    dot_general x6, matrix products, local_solve(): lax.dot_general(design, residual.astype(jnp.bfloat16), (((0,), (0,)), (()...  183 us
    psum x1, waiting for transfers between devices, local_solve(): residual = targets - lax.psum(partial, 'feat')  143 us
    sub x3, other arithmetic, local_solve(): residual = residual - MIX_WEIGHT * lax.psum(contrib, 'feat')  54.7 us
    dot_general x1, matrix products, local_solve(): jnp.dot(design, weights.astype(jnp.bfloat16), preferred_element_type=jnp....  34.7 us
  transfers between devices with their start and end apart: 7, of which 7 were waited for; matrix products, arithmetic and copies ran while one was open for 0% of the time, Pallas kernels for 0%

commit v1 on v0

v1 whole, which is shorter than its diff:
```python
import functools

import jax
import jax.numpy as jnp
from jax import lax
from jax.experimental import pallas as pl
from jax.experimental.pallas import tpu as pltpu
from jax.sharding import PartitionSpec as P

SWEEPS = 6
RIDGE_COEF = 1.0
MIX_WEIGHT = 0.75

UNITS = 16
RING = 4
CORES = 2
DEPTH = 8
PHASES = 2 * (SWEEPS + 1)
MESH = pl.DeviceIdType.MESH

PAIR_SEND, PAIR_WAIT = 1, 2
ONE_SEND, ONE_WAIT = 3, 5
TWO_SEND, TWO_WAIT = 6, 8
NEAR_SEND, NEAR_WAIT = 9, 11
FAR_WAIT = 14
TWIN_WAIT = 16
OUT_WAIT = 17

PAIR, ONE_R, ONE_L, TWO_R, TWO_L, NEAR_R, NEAR_L, FAR_R, FAR_L, TWIN = range(10)


def _solve(targets_k, half, top, x_hbm, y_hbm, w_hbm, eta_ref, w_out, r_out,
           xbuf, contrib, pair_in, one_r, one_l, two_r, two_l, own, in1_r, in1_l, in2_r, in2_l,
           shard, gathered, gathered_f32, weights, update, gradient,
           x_sem, y_sem, w_sem, out_sem, send_sem, recv_sem):
    samples = x_hbm.shape[0]
    rows = samples // UNITS
    lanes = rows // (RING * CORES)
    low = half - top
    rest = targets_k - half
    units = PHASES * UNITS
    ridge_val = RIDGE_COEF / samples

    feat = lax.axis_index('feat')
    chip = lax.div(feat, CORES)
    core = lax.rem(feat, CORES)
    twin = 1 - core
    right = lax.rem(chip + 1 + 2 * core, RING)
    left = lax.rem(chip + 3 - 2 * core, RING)
    opposite = lax.rem(chip + 2, RING)

    def device(q, j):
        return {'feat': q * CORES + j}

    to_right, to_left, to_twin = device(right, core), device(left, core), device(chip, twin)

    barrier = pltpu.get_barrier_semaphore()
    for target in (to_right, to_left, to_twin):
        pl.semaphore_signal(barrier, inc=1, device_id=target, device_id_type=MESH)
    pl.semaphore_wait(barrier, 3)

    def remote(kind, u, src, dst, target):
        slot = lax.rem(u, DEPTH)
        return pltpu.make_async_remote_copy(
            src_ref=src, dst_ref=dst, send_sem=send_sem.at[kind, slot], recv_sem=recv_sem.at[kind, slot],
            device_id=target, device_id_type=MESH)

    def slot_of(u):
        return lax.rem(u, UNITS)

    def half_of(u):
        return lax.rem(lax.div(u, UNITS), 2)

    def pair_copy(u):
        c = slot_of(u)
        return [remote(PAIR, u, contrib.at[c, twin], pair_in.at[c], to_twin)]

    def one_copies(u):
        c = slot_of(u)
        return [remote(ONE_R, u, one_r.at[c], in1_r.at[c], to_right),
                remote(ONE_L, u, one_l.at[c], in1_l.at[c], to_left)]

    def two_copies(u):
        c = slot_of(u)
        return [remote(TWO_R, u, two_r.at[c], in2_r.at[c], to_right),
                remote(TWO_L, u, two_l.at[c], in2_l.at[c], to_left)]

    def near_copies(u, buf):
        piece = buf.at[slot_of(u), core, chip]
        return [remote(NEAR_R, u, piece, piece, to_right), remote(NEAR_L, u, piece, piece, to_left)]

    def far_copies(u, buf):
        c = slot_of(u)
        from_left = buf.at[c, core, left, pl.ds(0, top)]
        from_right = buf.at[c, core, right, pl.ds(top, low)]
        return [remote(FAR_R, u, from_left, from_left, to_right), remote(FAR_L, u, from_right, from_right, to_left)]

    def twin_copy(u, buf):
        piece = buf.at[slot_of(u), core]
        return [remote(TWIN, u, piece, piece, to_twin)]

    def out_copies(u, h):
        c = slot_of(u)
        count = half if h == 0 else rest
        copies = []
        for p in range(RING * CORES):
            start = pl.multiple_of(c * rows + p * lanes, lanes)
            copies.append(pltpu.make_async_copy(
                gathered_f32.at[c, p // RING, p % RING, pl.ds(0, count)],
                r_out.at[pl.ds(h * half, count), pl.ds(start, lanes)], out_sem.at[p]))
        return copies

    def x_copy(s):
        start = pl.multiple_of(lax.rem(s, UNITS) * rows, rows)
        return pltpu.make_async_copy(x_hbm.at[pl.ds(start, rows)], xbuf.at[lax.rem(s, 2)], x_sem.at[lax.rem(s, 2)])

    def start_all(copies):
        for copy in copies:
            copy.start()

    def wait_all(copies):
        for copy in copies:
            copy.wait()

    def stage(s, offset, action):
        u = s - offset

        @pl.when(jnp.logical_and(u >= 0, u < units))
        def _():
            action(u)

    def stage_typed(s, offset, action):
        u = s - offset
        last = units - 2 * UNITS

        @pl.when(jnp.logical_and(u >= 0, u < last))
        def _():
            action(u, gathered)

        @pl.when(jnp.logical_and(u >= last, u < units))
        def _():
            action(u, gathered_f32)

    def final_stage(s, offset, action):
        u = s - offset
        for h in range(2):
            first = units - (2 - h) * UNITS

            @pl.when(jnp.logical_and(u >= first, u < first + UNITS))
            def _():
                action(out_copies(u, h))

    def sends(s):
        stage(s, PAIR_SEND, lambda u: start_all(pair_copy(u)))
        stage(s, TWO_SEND, lambda u: start_all(two_copies(u)))
        stage_typed(s, NEAR_SEND, lambda u, buf: start_all(near_copies(u, buf)))
        stage(s, ONE_SEND, lambda u: start_all(one_copies(u)))

    def waits(s):
        def relay(u, buf):
            wait_all(near_copies(u, buf))
            start_all(far_copies(u, buf))

        def share(u, buf):
            wait_all(far_copies(u, buf))
            start_all(twin_copy(u, buf))

        stage_typed(s, NEAR_WAIT, relay)
        stage_typed(s, FAR_WAIT, share)
        stage(s, PAIR_WAIT, lambda u: wait_all(pair_copy(u)))
        stage(s, ONE_WAIT, lambda u: wait_all(one_copies(u)))
        stage(s, TWO_WAIT, lambda u: wait_all(two_copies(u)))
        stage_typed(s, TWIN_WAIT, lambda u, buf: wait_all(twin_copy(u, buf)))
        final_stage(s, OUT_WAIT, wait_all)
        final_stage(s, TWIN_WAIT, start_all)

    def reduce(s):
        c = lax.rem(s + UNITS - PAIR_WAIT, UNITS)

        def pair_sum(q, start, count):
            return contrib[c, core, q, pl.ds(start, count)] + pair_in[c, q, pl.ds(start, count)]

        one_r[c, pl.ds(0, low)] = pair_sum(opposite, top, low)
        one_r[c, pl.ds(low, top)] = pair_sum(right, 0, top)
        one_l[c, pl.ds(0, top)] = pair_sum(opposite, 0, top)
        one_l[c, pl.ds(top, low)] = pair_sum(left, top, low)
        two_r[c] = pair_sum(right, top, low)
        two_l[c] = pair_sum(left, 0, top)
        own[c] = pair_sum(chip, 0, half)

        c = lax.rem(s + UNITS - ONE_WAIT, UNITS)
        two_r[c] = two_r[c] + in1_r[c, pl.ds(0, low)]
        two_l[c] = two_l[c] + in1_l[c, pl.ds(0, top)]

        u = s - TWO_WAIT
        c = lax.rem(s + UNITS - TWO_WAIT, UNITS)
        h = lax.rem(lax.div(s + 2 * UNITS - TWO_WAIT, UNITS), 2)
        valid = jnp.logical_and(u >= 0, u < units)
        coef = jnp.where(u < 2 * UNITS, 1.0, MIX_WEIGHT).astype(jnp.float32)
        for start, count, ring_sum in (
                (0, top, in1_r[c, pl.ds(low, top)] + in2_l[c]),
                (top, low, in1_l[c, pl.ds(top, low)] + in2_r[c])):
            old = shard[h, c, pl.ds(start, count)]
            total = own[c, pl.ds(start, count)] + ring_sum
            new = jnp.where(valid, old - coef * total, old)
            shard[h, c, pl.ds(start, count)] = new
            gathered_f32[c, core, chip, pl.ds(start, count)] = new
            gathered[c, core, chip, pl.ds(start, count)] = new.astype(jnp.bfloat16)

    x_copy(0).start()
    w_copies = [
        pltpu.make_async_copy(w_hbm.at[pl.ds(0, half)], weights.at[0], w_sem.at[0]),
        pltpu.make_async_copy(w_hbm.at[pl.ds(half, rest)], weights.at[1, pl.ds(0, rest)], w_sem.at[1])]
    start_all(w_copies)

    def y_copies(c):
        start = pl.multiple_of(c * rows + (core * RING + chip) * lanes, lanes)
        return [
            pltpu.make_async_copy(y_hbm.at[pl.ds(0, half), pl.ds(start, lanes)], shard.at[0, c], y_sem.at[0, c]),
            pltpu.make_async_copy(
                y_hbm.at[pl.ds(half, rest), pl.ds(start, lanes)], shard.at[1, c, pl.ds(0, rest)], y_sem.at[1, c])]

    for c in range(UNITS):
        start_all(y_copies(c))
    if rest < half:
        weights[1, pl.ds(rest, half - rest)] = jnp.zeros((half - rest, weights.shape[2]), jnp.float32)
        shard[1, :, pl.ds(rest, half - rest)] = jnp.zeros((UNITS, half - rest, lanes), jnp.float32)
    wait_all(w_copies)
    for h in range(2):
        update[h] = weights[h].astype(jnp.bfloat16)
    for c in range(UNITS):
        wait_all(y_copies(c))

    def main_step(s, carry):
        @pl.when(s + 1 < units)
        def _():
            x_copy(s + 1).start()

        sends(s)
        waits(s)
        x_copy(s).wait()

        c = slot_of(s)
        h = half_of(s)
        x = xbuf.at[lax.rem(s, 2)]
        product = lax.dot_general(update[h], x[...], (((1,), (1,)), ((), ())), preferred_element_type=jnp.float32)
        for p in range(RING * CORES):
            contrib[c, p // RING, p % RING] = product[:, p * lanes:(p + 1) * lanes]
        residual = jnp.concatenate(
            [gathered[c, p // RING, p % RING] for p in range(RING * CORES)], axis=1)
        term = jnp.dot(residual, x[...], preferred_element_type=jnp.float32)
        gradient[...] = jnp.where(c == 0, 0.0, gradient[...]) + term
        reduce(s)

        @pl.when(jnp.logical_and(c == UNITS - 1, jnp.logical_and(s >= UNITS, s < units - UNITS)))
        def _():
            w = weights[1 - h]
            step = eta_ref[...] * (gradient[...] / samples - ridge_val * w)
            weights[1 - h] = w + MIX_WEIGHT * step
            update[1 - h] = step.astype(jnp.bfloat16)

        return carry

    lax.fori_loop(0, units, main_step, 0)

    w_copies = [
        pltpu.make_async_copy(weights.at[0], w_out.at[pl.ds(0, half)], w_sem.at[0]),
        pltpu.make_async_copy(weights.at[1, pl.ds(0, rest)], w_out.at[pl.ds(half, rest)], w_sem.at[1])]
    start_all(w_copies)

    def drain_step(s, carry):
        sends(s)
        waits(s)
        reduce(s)
        return carry

    lax.fori_loop(units, units + OUT_WAIT, drain_step, 0)
    wait_all(w_copies)


def solution(mesh):
    def local_solve(design, targets, weights, step_sizes):
        samples, depth = design.shape
        k = targets.shape[1]
        half = 8 * pl.cdiv(pl.cdiv(k, 8), 2)
        top = half // 2 // 16 * 16
        low = half - top
        rows = samples // UNITS
        lanes = rows // (RING * CORES)
        assert mesh.shape['feat'] == RING * CORES and UNITS * RING * CORES * lanes == samples
        f32, bf16 = jnp.float32, jnp.bfloat16
        hbm = pl.BlockSpec(memory_space=pl.ANY)
        w_t, r_t = pl.pallas_call(
            functools.partial(_solve, k, half, top),
            out_shape=(jax.ShapeDtypeStruct((k, depth), f32), jax.ShapeDtypeStruct((k, samples), f32)),
            in_specs=[hbm, hbm, hbm, pl.BlockSpec(memory_space=pltpu.VMEM)],
            out_specs=(hbm, hbm),
            scratch_shapes=[
                pltpu.VMEM((2, rows, depth), bf16),
                pltpu.VMEM((UNITS, CORES, RING, half, lanes), f32),
                pltpu.VMEM((UNITS, RING, half, lanes), f32),
                pltpu.VMEM((UNITS, half, lanes), f32),
                pltpu.VMEM((UNITS, half, lanes), f32),
                pltpu.VMEM((UNITS, low, lanes), f32),
                pltpu.VMEM((UNITS, top, lanes), f32),
                pltpu.VMEM((UNITS, half, lanes), f32),
                pltpu.VMEM((UNITS, half, lanes), f32),
                pltpu.VMEM((UNITS, half, lanes), f32),
                pltpu.VMEM((UNITS, low, lanes), f32),
                pltpu.VMEM((UNITS, top, lanes), f32),
                pltpu.VMEM((2, UNITS, half, lanes), f32),
                pltpu.VMEM((UNITS, CORES, RING, half, lanes), bf16),
                pltpu.VMEM((UNITS, CORES, RING, half, lanes), f32),
                pltpu.VMEM((2, half, depth), f32),
                pltpu.VMEM((2, half, depth), bf16),
                pltpu.VMEM((half, depth), f32),
                pltpu.SemaphoreType.DMA((2,)),
                pltpu.SemaphoreType.DMA((2, UNITS)),
                pltpu.SemaphoreType.DMA((2,)),
                pltpu.SemaphoreType.DMA((RING * CORES,)),
                pltpu.SemaphoreType.DMA((10, DEPTH)),
                pltpu.SemaphoreType.DMA((10, DEPTH)),
            ],
            compiler_params=pltpu.CompilerParams(
                collective_id=0, has_side_effects=True, vmem_limit_bytes=62 * 1024 * 1024),
        )(design, targets.T, weights.T, step_sizes[None, :])
        return w_t.T, r_t.T

    return jax.shard_map(
        local_solve,
        mesh=mesh,
        in_specs=(P('prob', 'feat'), P('prob', None), P(('prob', 'feat'), None), P(('prob', 'feat'))),
        out_specs=(P(('prob', 'feat'), None), P('prob', None)),
        check_vma=False,
    )
```

time: 1490 us -> 646 us (0.43)
  waiting for transfers between devices: 985 us -> 0 us
  Pallas kernels: 0 us -> 631 us
  matrix products: 414 us -> 0 us
  other arithmetic: 69.1 us -> 0 us
    psum x7 -> x0, waiting for transfers between devices: 984 us -> none  [the longest x6 841 us: local_solve(): residual = residual - MIX_WEIGHT * lax.psum(contrib, 'feat')]
    pallas_call x0 -> x1, Pallas kernels: none -> 631 us  [local_solve(): pl.pallas_call(functools.partial(_solve, k, half, top), out_shape=(jax.Sh...]
    dot_general x13 -> x0, matrix products: 414 us -> none  [the longest x6 196 us: local_solve(): jnp.dot(design, update.astype(jnp.bfloat16), preferred_element_type=jnp.f...]
    sub x4 -> x0, other arithmetic: 69.1 us -> none  [the longest x3 54.7 us: local_solve(): residual = residual - MIX_WEIGHT * lax.psum(contrib, 'feat')]
  transfers between devices with their start and end apart: 7 -> 0, of which waited for: 7 -> 0; matrix products, arithmetic and copies ran while one was open for 0% -> 0% of each run, Pallas kernels for 0% -> 0%
where the time goes in v1:
time: 646 us
  Pallas kernels  631 us (98%)
  local copies, waits for them, and re-layouts  13.7 us (2%)
    pallas_call x1, Pallas kernels, local_solve(): pl.pallas_call(functools.partial(_solve, k, half, top), out_shape=(jax.Sh...  631 us
    unnamed x2, local copies, waits for them, and re-layouts  13.7 us

profile of v1, /device:TPU:113, one launch (start us, length us, event | category | flops | bytes accessed | tf_op | source)
XLA Modules:
  0.0 645.8 jit_solution(17207473149007969596)
XLA Ops:
  0.6 631.4 %shard_map.59 = (f32[200,2048]{1,0:T(8,128)}, f32[200,16384]{1,0:T(8,128)}) custom-call(bf16[16384,2048]{1,0:T(8,128)(2,1)} %x_hbm.1, f32[200,16384]{1,0:T(8,128)} %bitcast.5, f32[200,2048]{1,0:T(8,128)} %bitcast.7, f32[1,2048]{1,0:T(1,128)} %bitcast.9), custom_call_target="tpu_custom_call" | custom-call | tf_op jit(solution)/shard_map/pallas_call | solution.py:293
  632.1 2.8 copy.8
  634.8 11.0 %copy.9 = f32[16384,200]{0,1:T(8,128)} copy(f32[16384,200]{0,1:T(8,128)} %bitcast.6) | data formatting | bytes 26214400

commit v2 on v1

v2 whole, which is shorter than its diff:
```python
import functools

import jax
import jax.numpy as jnp
from jax import lax
from jax.experimental import pallas as pl
from jax.experimental.pallas import tpu as pltpu
from jax.sharding import PartitionSpec as P

SWEEPS = 6
RIDGE_COEF = 1.0
MIX_WEIGHT = 0.75

UNITS = 16
RING = 4
CORES = 2
DEPTH = 8
PHASES = 2 * (SWEEPS + 1)
MESH = pl.DeviceIdType.MESH

PAIR_SEND, PAIR_WAIT = 1, 2
ONE_SEND, ONE_WAIT = 3, 5
TWO_SEND, TWO_WAIT = 6, 8
NEAR_SEND, NEAR_WAIT = 9, 11
FAR_WAIT = 14
TWIN_WAIT = 16

PAIR, ONE_R, ONE_L, TWO_R, TWO_L, NEAR_R, NEAR_L, FAR_R, FAR_L, TWIN = range(10)


def _solve(targets_k, half, top, x_hbm, y_hbm, w_hbm, eta_ref, w_out, r_out,
           xbuf, contrib, pair_in, one_r, one_l, two_r, two_l, own, in1_r, in1_l, in2_r, in2_l,
           shard, gathered, weights, update, gradient,
           x_sem, y_sem, w_sem, out_sem, send_sem, recv_sem):
    samples = x_hbm.shape[0]
    rows = samples // UNITS
    lanes = rows // (RING * CORES)
    low = half - top
    rest = targets_k - half
    units = PHASES * UNITS
    ridge_val = RIDGE_COEF / samples

    feat = lax.axis_index('feat')
    chip = lax.div(feat, CORES)
    core = lax.rem(feat, CORES)
    twin = 1 - core
    right = lax.rem(chip + 1 + 2 * core, RING)
    left = lax.rem(chip + 3 - 2 * core, RING)
    opposite = lax.rem(chip + 2, RING)

    def device(q, j):
        return {'feat': q * CORES + j}

    to_right, to_left, to_twin = device(right, core), device(left, core), device(chip, twin)

    def remote(kind, u, src, dst, target):
        slot = lax.rem(u, DEPTH)
        return pltpu.make_async_remote_copy(
            src_ref=src, dst_ref=dst, send_sem=send_sem.at[kind, slot], recv_sem=recv_sem.at[kind, slot],
            device_id=target, device_id_type=MESH)

    def slot_of(u):
        return lax.rem(u, UNITS)

    def half_of(u):
        return lax.rem(lax.div(u, UNITS), 2)

    def count_of(h):
        return half if h == 0 else rest

    def columns(c, j, q, pieces=1):
        return pl.ds(pl.multiple_of(c * rows + (j * RING + q) * lanes, lanes), pieces * lanes)

    def pair_copy(u, h):
        c, part = slot_of(u), pl.ds(0, count_of(h))
        return [remote(PAIR, u, contrib.at[c, twin, :, part], pair_in.at[c, :, part], to_twin)]

    def one_copies(u, h):
        c, part = slot_of(u), pl.ds(0, count_of(h))
        return [remote(ONE_R, u, one_r.at[c, part], in1_r.at[c, part], to_right),
                remote(ONE_L, u, one_l.at[c, part], in1_l.at[c, part], to_left)]

    def two_copies(u, h):
        c, part = slot_of(u), pl.ds(0, count_of(h) - top)
        return [remote(TWO_R, u, two_r.at[c, part], in2_r.at[c, part], to_right),
                remote(TWO_L, u, two_l.at[c], in2_l.at[c], to_left)]

    def place(u, h, last, q, start, count):
        c = slot_of(u)
        if last:
            return r_out.at[pl.ds(h * half + start, count), columns(c, core, q)]
        return gathered.at[c, core, q, pl.ds(start, count)]

    def near_copies(u, h, last):
        piece = place(u, h, last, chip, 0, count_of(h))
        source = shard.at[h, slot_of(u), pl.ds(0, count_of(h))] if last else piece
        return [remote(NEAR_R, u, source, piece, to_right), remote(NEAR_L, u, source, piece, to_left)]

    def own_copy(u, h):
        return [pltpu.make_async_copy(
            shard.at[h, slot_of(u), pl.ds(0, count_of(h))], place(u, h, True, chip, 0, count_of(h)),
            out_sem.at[lax.rem(u, DEPTH)])]

    def far_copies(u, h, last):
        from_left = place(u, h, last, left, 0, top)
        from_right = place(u, h, last, right, top, count_of(h) - top)
        return [remote(FAR_R, u, from_left, from_left, to_right), remote(FAR_L, u, from_right, from_right, to_left)]

    def twin_copy(u, h, last):
        c = slot_of(u)
        if last:
            piece = r_out.at[pl.ds(h * half, count_of(h)), columns(c, core, 0, RING)]
        else:
            piece = gathered.at[c, core, :, pl.ds(0, count_of(h))]
        return [remote(TWIN, u, piece, piece, to_twin)]

    def x_copy(s):
        start = pl.multiple_of(lax.rem(s, UNITS) * rows, rows)
        return pltpu.make_async_copy(x_hbm.at[pl.ds(start, rows)], xbuf.at[lax.rem(s, 2)], x_sem.at[lax.rem(s, 2)])

    def start_all(copies):
        for copy in copies:
            copy.start()

    def wait_all(copies):
        for copy in copies:
            copy.wait()

    def stage(s, offset, action):
        u = s - offset
        valid = jnp.logical_and(u >= 0, u < units)
        for h in range(2):
            @pl.when(jnp.logical_and(valid, half_of(u) == h))
            def _():
                action(u, h)

    def stage_typed(s, offset, action):
        u = s - offset
        final = units - 2 * UNITS
        for h in range(2):
            @pl.when(jnp.logical_and(jnp.logical_and(u >= 0, u < final), half_of(u) == h))
            def _():
                action(u, h, False)

            first = final + h * UNITS

            @pl.when(jnp.logical_and(u >= first, u < first + UNITS))
            def _():
                action(u, h, True)

    def sends(s):
        def near(u, h, last):
            start_all(near_copies(u, h, last))
            if last:
                start_all(own_copy(u, h))

        stage(s, PAIR_SEND, lambda u, h: start_all(pair_copy(u, h)))
        stage(s, TWO_SEND, lambda u, h: start_all(two_copies(u, h)))
        stage_typed(s, NEAR_SEND, near)
        stage(s, ONE_SEND, lambda u, h: start_all(one_copies(u, h)))

    def waits(s):
        def relay(u, h, last):
            wait_all(near_copies(u, h, last))
            start_all(far_copies(u, h, last))

        def share(u, h, last):
            wait_all(far_copies(u, h, last))
            if last:
                wait_all(own_copy(u, h))
            start_all(twin_copy(u, h, last))

        stage_typed(s, NEAR_WAIT, relay)
        stage_typed(s, FAR_WAIT, share)
        stage(s, PAIR_WAIT, lambda u, h: wait_all(pair_copy(u, h)))
        stage(s, ONE_WAIT, lambda u, h: wait_all(one_copies(u, h)))
        stage(s, TWO_WAIT, lambda u, h: wait_all(two_copies(u, h)))
        stage_typed(s, TWIN_WAIT, lambda u, h, last: wait_all(twin_copy(u, h, last)))

    def reduce(s):
        c = lax.rem(s + UNITS - PAIR_WAIT, UNITS)

        def pair_sum(q, start, count):
            return contrib[c, core, q, pl.ds(start, count)] + pair_in[c, q, pl.ds(start, count)]

        one_r[c, pl.ds(0, top)] = pair_sum(right, 0, top)
        one_r[c, pl.ds(top, low)] = pair_sum(opposite, top, low)
        one_l[c, pl.ds(0, top)] = pair_sum(opposite, 0, top)
        one_l[c, pl.ds(top, low)] = pair_sum(left, top, low)
        two_r[c] = pair_sum(right, top, low)
        two_l[c] = pair_sum(left, 0, top)
        own[c] = pair_sum(chip, 0, half)

        c = lax.rem(s + UNITS - ONE_WAIT, UNITS)
        two_r[c] = two_r[c] + in1_r[c, pl.ds(top, low)]
        two_l[c] = two_l[c] + in1_l[c, pl.ds(0, top)]

        u = s - TWO_WAIT
        c = lax.rem(s + UNITS - TWO_WAIT, UNITS)
        h = lax.rem(lax.div(s + 2 * UNITS - TWO_WAIT, UNITS), 2)
        valid = jnp.logical_and(u >= 0, u < units)
        coef = jnp.where(u < 2 * UNITS, 1.0, MIX_WEIGHT).astype(jnp.float32)
        for start, count, ring_sum in (
                (0, top, in1_r[c, pl.ds(0, top)] + in2_l[c]),
                (top, low, in1_l[c, pl.ds(top, low)] + in2_r[c])):
            old = shard[h, c, pl.ds(start, count)]
            total = own[c, pl.ds(start, count)] + ring_sum
            new = jnp.where(valid, old - coef * total, old)
            shard[h, c, pl.ds(start, count)] = new
            gathered[c, core, chip, pl.ds(start, count)] = new.astype(jnp.bfloat16)

    x_copy(0).start()
    w_copies = [
        pltpu.make_async_copy(w_hbm.at[pl.ds(0, half)], weights.at[0], w_sem.at[0]),
        pltpu.make_async_copy(w_hbm.at[pl.ds(half, rest)], weights.at[1, pl.ds(0, rest)], w_sem.at[1])]
    start_all(w_copies)

    def y_copies(c):
        start = pl.multiple_of(c * rows + (core * RING + chip) * lanes, lanes)
        return [
            pltpu.make_async_copy(y_hbm.at[pl.ds(0, half), pl.ds(start, lanes)], shard.at[0, c], y_sem.at[0, c]),
            pltpu.make_async_copy(
                y_hbm.at[pl.ds(half, rest), pl.ds(start, lanes)], shard.at[1, c, pl.ds(0, rest)], y_sem.at[1, c])]

    for c in range(UNITS):
        start_all(y_copies(c))
    if rest < half:
        weights[1, pl.ds(rest, half - rest)] = jnp.zeros((half - rest, weights.shape[2]), jnp.float32)
        shard[1, :, pl.ds(rest, half - rest)] = jnp.zeros((UNITS, half - rest, lanes), jnp.float32)
    barrier = pltpu.get_barrier_semaphore()
    for target in (to_right, to_left, to_twin):
        pl.semaphore_signal(barrier, inc=1, device_id=target, device_id_type=MESH)
    pl.semaphore_wait(barrier, 3)

    wait_all(w_copies)
    for h in range(2):
        update[h] = weights[h].astype(jnp.bfloat16)
    for c in range(UNITS):
        wait_all(y_copies(c))

    def main_step(s, carry, with_gradient):
        @pl.when(s + 1 < units)
        def _():
            x_copy(s + 1).start()

        sends(s)
        waits(s)
        x_copy(s).wait()

        c = slot_of(s)
        h = half_of(s)
        x = xbuf.at[lax.rem(s, 2)]
        product = lax.dot_general(update[h], x[...], (((1,), (1,)), ((), ())), preferred_element_type=jnp.float32)
        for p in range(RING * CORES):
            contrib[c, p // RING, p % RING] = product[:, p * lanes:(p + 1) * lanes]
        if with_gradient:
            residual = jnp.concatenate(
                [gathered[c, p // RING, p % RING] for p in range(RING * CORES)], axis=1)
            term = jnp.dot(residual, x[...], preferred_element_type=jnp.float32)
            gradient[...] = jnp.where(c == 0, 0.0, gradient[...]) + term
        reduce(s)
        if not with_gradient:
            return carry

        @pl.when(c == UNITS - 1)
        def _():
            w = weights[1 - h]
            step = eta_ref[...] * (gradient[...] / samples - ridge_val * w)
            weights[1 - h] = w + MIX_WEIGHT * step
            update[1 - h] = step.astype(jnp.bfloat16)

        return carry

    no_gradient = functools.partial(main_step, with_gradient=False)
    lax.fori_loop(0, UNITS, no_gradient, 0)
    lax.fori_loop(UNITS, units - UNITS, functools.partial(main_step, with_gradient=True), 0)
    lax.fori_loop(units - UNITS, units, no_gradient, 0)

    w_copies = [
        pltpu.make_async_copy(weights.at[0], w_out.at[pl.ds(0, half)], w_sem.at[0]),
        pltpu.make_async_copy(weights.at[1, pl.ds(0, rest)], w_out.at[pl.ds(half, rest)], w_sem.at[1])]
    start_all(w_copies)

    def drain_step(s, carry):
        sends(s)
        waits(s)
        reduce(s)
        return carry

    lax.fori_loop(units, units + TWIN_WAIT, drain_step, 0)
    wait_all(w_copies)


def _store(w_in, r_in, w_out, r_out, sems):
    parts = sems.shape[0] - 1
    width = r_in.shape[1] // parts
    copies = [pltpu.make_async_copy(w_in, w_out, sems.at[parts])]
    for p in range(parts):
        part = pl.ds(p * width, width)
        copies.append(pltpu.make_async_copy(r_in.at[:, part], r_out.at[:, part], sems.at[p]))
    for copy in copies:
        copy.start()
    for copy in copies:
        copy.wait()


def solution(mesh):
    def local_solve(design, targets, weights, step_sizes):
        samples, depth = design.shape
        k = targets.shape[1]
        half = 8 * pl.cdiv(pl.cdiv(k, 8), 2)
        top = half // 2 // 16 * 16
        low = half - top
        rows = samples // UNITS
        lanes = rows // (RING * CORES)
        assert mesh.shape['feat'] == RING * CORES and UNITS * RING * CORES * lanes == samples
        f32, bf16 = jnp.float32, jnp.bfloat16
        hbm = pl.BlockSpec(memory_space=pltpu.HBM)
        anywhere = pl.BlockSpec(memory_space=pl.ANY)
        w_t, r_t = pl.pallas_call(
            functools.partial(_solve, k, half, top),
            out_shape=(jax.ShapeDtypeStruct((k, depth), f32), jax.ShapeDtypeStruct((k, samples), f32)),
            in_specs=[hbm, hbm, hbm, pl.BlockSpec(memory_space=pltpu.VMEM)],
            out_specs=(anywhere, anywhere),
            scratch_shapes=[
                pltpu.VMEM((2, rows, depth), bf16),
                pltpu.VMEM((UNITS, CORES, RING, half, lanes), f32),
                pltpu.VMEM((UNITS, RING, half, lanes), f32),
                pltpu.VMEM((UNITS, half, lanes), f32),
                pltpu.VMEM((UNITS, half, lanes), f32),
                pltpu.VMEM((UNITS, low, lanes), f32),
                pltpu.VMEM((UNITS, top, lanes), f32),
                pltpu.VMEM((UNITS, half, lanes), f32),
                pltpu.VMEM((UNITS, half, lanes), f32),
                pltpu.VMEM((UNITS, half, lanes), f32),
                pltpu.VMEM((UNITS, low, lanes), f32),
                pltpu.VMEM((UNITS, top, lanes), f32),
                pltpu.VMEM((2, UNITS, half, lanes), f32),
                pltpu.VMEM((UNITS, CORES, RING, half, lanes), bf16),
                pltpu.VMEM((2, half, depth), f32),
                pltpu.VMEM((2, half, depth), bf16),
                pltpu.VMEM((half, depth), f32),
                pltpu.SemaphoreType.DMA((2,)),
                pltpu.SemaphoreType.DMA((2, UNITS)),
                pltpu.SemaphoreType.DMA((2,)),
                pltpu.SemaphoreType.DMA((DEPTH,)),
                pltpu.SemaphoreType.DMA((10, DEPTH)),
                pltpu.SemaphoreType.DMA((10, DEPTH)),
            ],
            compiler_params=pltpu.CompilerParams(
                collective_id=0, has_side_effects=True, vmem_limit_bytes=36 * 1024 * 1024),
        )(design, targets.T, weights.T, step_sizes[None, :])
        w_t, r_t = pl.pallas_call(
            _store,
            out_shape=(jax.ShapeDtypeStruct((k, depth), f32), jax.ShapeDtypeStruct((k, samples), f32)),
            in_specs=[anywhere, anywhere],
            out_specs=(hbm, hbm),
            scratch_shapes=[pltpu.SemaphoreType.DMA((9,))],
            compiler_params=pltpu.CompilerParams(vmem_limit_bytes=1024 * 1024),
        )(w_t, r_t)
        return w_t.T, r_t.T

    return jax.shard_map(
        local_solve,
        mesh=mesh,
        in_specs=(P('prob', 'feat'), P('prob', None), P(('prob', 'feat'), None), P(('prob', 'feat'))),
        out_specs=(P(('prob', 'feat'), None), P('prob', None)),
        check_vma=False,
    )
```

time: 646 us -> 628 us (0.972)
  local copies, waits for them, and re-layouts: 13.7 us -> 2.12 us
    unnamed x2 -> x4, local copies, waits for them, and re-layouts: 13.7 us -> 2.12 us
    pallas_call x1, Pallas kernels: 631 us -> 620 us  [local_solve(): pl.pallas_call(functools.partial(_solve, k, half, top), out_shape=(jax.Sh...]
where the time goes in v2:
time: 628 us
  Pallas kernels  625 us (100%)
    pallas_call x1, Pallas kernels, local_solve(): pl.pallas_call(functools.partial(_solve, k, half, top), out_shape=(jax.Sh...  620 us

profile of v2, /device:TPU:113, one launch (start us, length us, event | category | flops | bytes accessed | tf_op | source)
XLA Modules:
  0.0 627.9 jit_solution(13841221950740177596)
XLA Ops:
  0.6 0.0 copy-start
  0.6 1.4 copy-done
  2.1 0.0 copy-start.1
  2.1 0.7 copy-done.1
  2.8 619.8 %shard_map.59 = (f32[200,2048]{1,0:T(8,128)S(1)}, f32[200,16384]{1,0:T(8,128)S(1)}) custom-call(bf16[16384,2048]{1,0:T(8,128)(2,1)} %x_hbm.1, f32[200,16384]{1,0:T(8,128)} %bitcast.7, f32[200,2048]{1,0:T(8,128)S(1)} %bitcast.5, f32[1,2048]{1,0:T(1,128)S(1)} %bitcast.6), custom_call_target="tpu_custom_call" | custom-call | tf_op jit(solution)/shard_map/pallas_call | solution.py:320
  622.6 5.3 shard_map.60
Async XLA Ops:
  0.6 1.4 copy-start
  2.1 0.7 copy-start.1

commit v3 on v2

v3 whole, which is shorter than its diff:
```python
import functools

import jax
import jax.numpy as jnp
from jax import lax
from jax.experimental import pallas as pl
from jax.experimental.pallas import tpu as pltpu
from jax.sharding import PartitionSpec as P

SWEEPS = 6
RIDGE_COEF = 1.0
MIX_WEIGHT = 0.75

UNITS = 16
RING = 4
CORES = 2
DEPTH = 8
PHASES = 2 * (SWEEPS + 1)
MESH = pl.DeviceIdType.MESH

PAIR_SEND, PAIR_WAIT = 1, 2
ONE_SEND, ONE_WAIT = 3, 6
TWO_SEND, TWO_WAIT = 7, 9
NEAR_SEND, NEAR_WAIT = 10, 12
FAR_WAIT = 14
TWIN_WAIT = UNITS

PAIR, ONE_R, ONE_L, TWO_R, TWO_L, NEAR_R, NEAR_L, FAR_R, FAR_L, TWIN = range(10)


def _solve(targets_k, half, top, x_hbm, y_hbm, w_hbm, eta_hbm, w_out, r_out,
           xbuf, contrib, pair_in, one_r, one_l, two_r, two_l, own, in1_r, in1_l, in2_r, in2_l,
           shard, gathered, weights, update, gradient, eta,
           x_sem, y_sem, w_sem, out_sem, send_sem, recv_sem):
    samples = x_hbm.shape[0]
    rows = samples // UNITS
    lanes = rows // (RING * CORES)
    low = half - top
    rest = targets_k - half
    ridge_val = RIDGE_COEF / samples

    feat = lax.axis_index('feat')
    chip = lax.div(feat, CORES)
    core = lax.rem(feat, CORES)
    twin = 1 - core
    right = lax.rem(chip + 1 + 2 * core, RING)
    left = lax.rem(chip + 3 - 2 * core, RING)
    opposite = lax.rem(chip + 2, RING)

    def device(q, j):
        return {'feat': q * CORES + j}

    to_right, to_left, to_twin = device(right, core), device(left, core), device(chip, twin)

    def unit_at(step, offset):
        phase, odd, c = step
        wrapped = c < offset
        return (phase - jnp.where(wrapped, 1, 0), jnp.where(wrapped, c + (UNITS - offset), c - offset),
                jnp.where(wrapped, 1 - odd, odd))

    def remote(kind, c, src, dst, target):
        sem = jnp.where(c >= DEPTH, c - DEPTH, c)
        return pltpu.make_async_remote_copy(
            src_ref=src, dst_ref=dst, send_sem=send_sem.at[kind, sem], recv_sem=recv_sem.at[kind, sem],
            device_id=target, device_id_type=MESH)

    def count_of(h):
        return half if h == 0 else rest

    def columns(c, j, q, pieces=1):
        return pl.ds(pl.multiple_of(c * rows + (j * RING + q) * lanes, lanes), pieces * lanes)

    def pair_copy(c, h):
        part = pl.ds(0, count_of(h))
        return [remote(PAIR, c, contrib.at[c, twin, :, part], pair_in.at[c, :, part], to_twin)]

    def one_copies(c, h):
        part = pl.ds(0, count_of(h))
        return [remote(ONE_R, c, one_r.at[c, part], in1_r.at[c, part], to_right),
                remote(ONE_L, c, one_l.at[c, part], in1_l.at[c, part], to_left)]

    def two_copies(c, h):
        part = pl.ds(0, count_of(h) - top)
        return [remote(TWO_R, c, two_r.at[c, part], in2_r.at[c, part], to_right),
                remote(TWO_L, c, two_l.at[c], in2_l.at[c], to_left)]

    def place(c, h, last, q, start, count):
        if last:
            return r_out.at[pl.ds(h * half + start, count), columns(c, core, q)]
        return gathered.at[c, core, q, pl.ds(start, count)]

    def near_copies(c, h, last):
        piece = place(c, h, last, chip, 0, count_of(h))
        source = shard.at[h, c, pl.ds(0, count_of(h))] if last else piece
        return [remote(NEAR_R, c, source, piece, to_right), remote(NEAR_L, c, source, piece, to_left)]

    def own_copy(c, h):
        return [pltpu.make_async_copy(
            shard.at[h, c, pl.ds(0, count_of(h))], place(c, h, True, chip, 0, count_of(h)),
            out_sem.at[c])]

    def far_copies(c, h, last):
        from_left = place(c, h, last, left, 0, top)
        from_right = place(c, h, last, right, top, count_of(h) - top)
        return [remote(FAR_R, c, from_left, from_left, to_right), remote(FAR_L, c, from_right, from_right, to_left)]

    def twin_copy(c, h, last):
        if last:
            piece = r_out.at[pl.ds(h * half, count_of(h)), columns(c, core, 0, RING)]
        else:
            piece = gathered.at[c, core, :, pl.ds(0, count_of(h))]
        return [remote(TWIN, c, piece, piece, to_twin)]

    def x_copy(c, buf):
        start = pl.multiple_of(c * rows, rows)
        return pltpu.make_async_copy(x_hbm.at[pl.ds(start, rows)], xbuf.at[buf], x_sem.at[buf])

    def start_all(copies):
        for copy in copies:
            copy.start()

    def wait_all(copies):
        for copy in copies:
            copy.wait()

    def stage(step, offset, action):
        phase, c, odd = unit_at(step, offset)
        valid = jnp.logical_and(phase >= 0, phase < PHASES)
        for h in range(2):
            @pl.when(jnp.logical_and(valid, odd == h))
            def _():
                action(c, h)

    def stage_typed(step, offset, action):
        phase, c, odd = unit_at(step, offset)
        rounded = jnp.logical_and(phase >= 0, phase < PHASES - 2)
        for h in range(2):
            @pl.when(jnp.logical_and(rounded, odd == h))
            def _():
                action(c, h, False)

            @pl.when(phase == PHASES - 2 + h)
            def _():
                action(c, h, True)

    def exchange(step):
        def near(c, h, last):
            start_all(near_copies(c, h, last))
            if last:
                start_all(own_copy(c, h))

        def relay(c, h, last):
            wait_all(near_copies(c, h, last))
            start_all(far_copies(c, h, last))

        def share(c, h, last):
            wait_all(far_copies(c, h, last))
            if last:
                wait_all(own_copy(c, h))
            start_all(twin_copy(c, h, last))

        stage(step, PAIR_SEND, lambda c, h: start_all(pair_copy(c, h)))
        stage_typed(step, NEAR_WAIT, relay)
        stage(step, TWO_SEND, lambda c, h: start_all(two_copies(c, h)))
        stage_typed(step, NEAR_SEND, near)
        stage(step, ONE_SEND, lambda c, h: start_all(one_copies(c, h)))
        stage_typed(step, FAR_WAIT, share)
        stage(step, PAIR_WAIT, lambda c, h: wait_all(pair_copy(c, h)))
        stage(step, TWO_WAIT, lambda c, h: wait_all(two_copies(c, h)))
        stage(step, ONE_WAIT, lambda c, h: wait_all(one_copies(c, h)))
        stage_typed(step, TWIN_WAIT, lambda c, h, last: wait_all(twin_copy(c, h, last)))

    def reduce(step):
        _, c, _ = unit_at(step, PAIR_WAIT)

        def pair_sum(q, start, count):
            return contrib[c, core, q, pl.ds(start, count)] + pair_in[c, q, pl.ds(start, count)]

        one_r[c, pl.ds(0, top)] = pair_sum(right, 0, top)
        one_r[c, pl.ds(top, low)] = pair_sum(opposite, top, low)
        one_l[c, pl.ds(0, top)] = pair_sum(opposite, 0, top)
        one_l[c, pl.ds(top, low)] = pair_sum(left, top, low)
        two_r[c] = pair_sum(right, top, low)
        two_l[c] = pair_sum(left, 0, top)
        own[c] = pair_sum(chip, 0, half)

        _, c, _ = unit_at(step, ONE_WAIT)
        two_r[c] = two_r[c] + in1_r[c, pl.ds(top, low)]
        two_l[c] = two_l[c] + in1_l[c, pl.ds(0, top)]

        phase, c, h = unit_at(step, TWO_WAIT)
        valid = jnp.logical_and(phase >= 0, phase < PHASES)
        coef = jnp.where(phase < 2, 1.0, MIX_WEIGHT).astype(jnp.float32)
        for start, count, ring_sum in (
                (0, top, in1_r[c, pl.ds(0, top)] + in2_l[c]),
                (top, low, in1_l[c, pl.ds(top, low)] + in2_r[c])):
            old = shard[h, c, pl.ds(start, count)]
            total = own[c, pl.ds(start, count)] + ring_sum
            new = jnp.where(valid, old - coef * total, old)
            shard[h, c, pl.ds(start, count)] = new
            gathered[c, core, chip, pl.ds(start, count)] = new.astype(jnp.bfloat16)

    x_copy(0, 0).start()
    eta_copy = pltpu.make_async_copy(eta_hbm, eta, w_sem.at[2])
    eta_copy.start()
    w_copies = [
        pltpu.make_async_copy(w_hbm.at[pl.ds(0, half)], weights.at[0], w_sem.at[0]),
        pltpu.make_async_copy(w_hbm.at[pl.ds(half, rest)], weights.at[1, pl.ds(0, rest)], w_sem.at[1])]
    start_all(w_copies)

    def y_copies(c):
        start = pl.multiple_of(c * rows + (core * RING + chip) * lanes, lanes)
        return [
            pltpu.make_async_copy(y_hbm.at[pl.ds(0, half), pl.ds(start, lanes)], shard.at[0, c], y_sem.at[0, c]),
            pltpu.make_async_copy(
                y_hbm.at[pl.ds(half, rest), pl.ds(start, lanes)], shard.at[1, c, pl.ds(0, rest)], y_sem.at[1, c])]

    for c in range(UNITS):
        start_all(y_copies(c))
    if rest < half:
        weights[1, pl.ds(rest, half - rest)] = jnp.zeros((half - rest, weights.shape[2]), jnp.float32)
        shard[1, :, pl.ds(rest, half - rest)] = jnp.zeros((UNITS, half - rest, lanes), jnp.float32)
    barrier = pltpu.get_barrier_semaphore()
    for target in (to_right, to_left, to_twin):
        pl.semaphore_signal(barrier, inc=1, device_id=target, device_id_type=MESH)
    pl.semaphore_wait(barrier, 3)

    wait_all(w_copies)
    eta_copy.wait()
    for h in range(2):
        update[h] = weights[h].astype(jnp.bfloat16)
    for c in range(UNITS):
        wait_all(y_copies(c))

    def main_step(phase, odd, with_gradient, more, c):
        step = (phase, odd, c)
        buf = lax.rem(c, 2)

        @pl.when(c < UNITS - 1)
        def _():
            x_copy(c + 1, 1 - buf).start()

        if more:
            @pl.when(c == UNITS - 1)
            def _():
                x_copy(0, 0).start()

        exchange(step)
        x_copy(c, buf).wait()

        x = xbuf.at[buf]
        product = lax.dot_general(update[odd], x[...], (((1,), (1,)), ((), ())), preferred_element_type=jnp.float32)
        for p in range(RING * CORES):
            contrib[c, p // RING, p % RING] = product[:, p * lanes:(p + 1) * lanes]
        if with_gradient:
            residual = jnp.concatenate(
                [gathered[c, p // RING, p % RING] for p in range(RING * CORES)], axis=1)
            term = jnp.dot(residual, x[...], preferred_element_type=jnp.float32)
            gradient[...] = jnp.where(c == 0, 0.0, gradient[...]) + term
        reduce(step)

    def run(phase, odd, with_gradient, more):
        def body(c, carry):
            main_step(phase, odd, with_gradient, more, c)
            return carry

        lax.fori_loop(0, UNITS, body, 0)

    def sweep_half(phase, carry):
        odd = lax.rem(phase, 2)
        run(phase, odd, True, True)
        w = weights[1 - odd]
        change = eta[...] * (gradient[...] / samples - ridge_val * w)
        weights[1 - odd] = w + MIX_WEIGHT * change
        update[1 - odd] = change.astype(jnp.bfloat16)
        return carry

    run(0, 0, False, True)
    lax.fori_loop(1, PHASES - 1, sweep_half, 0)
    run(PHASES - 1, 1, False, False)

    w_copies = [
        pltpu.make_async_copy(weights.at[0], w_out.at[pl.ds(0, half)], w_sem.at[0]),
        pltpu.make_async_copy(weights.at[1, pl.ds(0, rest)], w_out.at[pl.ds(half, rest)], w_sem.at[1])]
    start_all(w_copies)

    def drain_step(c, carry):
        exchange((PHASES, 0, c))
        reduce((PHASES, 0, c))
        return carry

    lax.fori_loop(0, UNITS, drain_step, 0)
    wait_all(w_copies)


def _store(w_in, r_in, w_out, r_out, sems):
    parts = sems.shape[0] - 1
    width = r_in.shape[1] // parts
    copies = [pltpu.make_async_copy(w_in, w_out, sems.at[parts])]
    for p in range(parts):
        part = pl.ds(p * width, width)
        copies.append(pltpu.make_async_copy(r_in.at[:, part], r_out.at[:, part], sems.at[p]))
    for copy in copies:
        copy.start()
    for copy in copies:
        copy.wait()


def solution(mesh):
    def local_solve(design, targets, weights, step_sizes):
        samples, depth = design.shape
        k = targets.shape[1]
        half = 8 * pl.cdiv(pl.cdiv(k, 8), 2)
        top = half // 2 // 16 * 16
        low = half - top
        rows = samples // UNITS
        lanes = rows // (RING * CORES)
        assert mesh.shape['feat'] == RING * CORES and UNITS * RING * CORES * lanes == samples
        f32, bf16 = jnp.float32, jnp.bfloat16
        hbm = pl.BlockSpec(memory_space=pltpu.HBM)
        anywhere = pl.BlockSpec(memory_space=pl.ANY)
        w_t, r_t = pl.pallas_call(
            functools.partial(_solve, k, half, top),
            out_shape=(jax.ShapeDtypeStruct((k, depth), f32), jax.ShapeDtypeStruct((k, samples), f32)),
            in_specs=[hbm, hbm, hbm, hbm],
            out_specs=(anywhere, anywhere),
            scratch_shapes=[
                pltpu.VMEM((2, rows, depth), bf16),
                pltpu.VMEM((UNITS, CORES, RING, half, lanes), f32),
                pltpu.VMEM((UNITS, RING, half, lanes), f32),
                pltpu.VMEM((UNITS, half, lanes), f32),
                pltpu.VMEM((UNITS, half, lanes), f32),
                pltpu.VMEM((UNITS, low, lanes), f32),
                pltpu.VMEM((UNITS, top, lanes), f32),
                pltpu.VMEM((UNITS, half, lanes), f32),
                pltpu.VMEM((UNITS, half, lanes), f32),
                pltpu.VMEM((UNITS, half, lanes), f32),
                pltpu.VMEM((UNITS, low, lanes), f32),
                pltpu.VMEM((UNITS, top, lanes), f32),
                pltpu.VMEM((2, UNITS, half, lanes), f32),
                pltpu.VMEM((UNITS, CORES, RING, half, lanes), bf16),
                pltpu.VMEM((2, half, depth), f32),
                pltpu.VMEM((2, half, depth), bf16),
                pltpu.VMEM((half, depth), f32),
                pltpu.VMEM((1, depth), f32),
                pltpu.SemaphoreType.DMA((2,)),
                pltpu.SemaphoreType.DMA((2, UNITS)),
                pltpu.SemaphoreType.DMA((3,)),
                pltpu.SemaphoreType.DMA((UNITS,)),
                pltpu.SemaphoreType.DMA((10, DEPTH)),
                pltpu.SemaphoreType.DMA((10, DEPTH)),
            ],
            compiler_params=pltpu.CompilerParams(
                collective_id=0, has_side_effects=True, vmem_limit_bytes=36 * 1024 * 1024),
        )(design, targets.T, pltpu.with_memory_space_constraint(weights.T, pltpu.HBM),
          pltpu.with_memory_space_constraint(step_sizes[None, :], pltpu.HBM))
        w_t, r_t = pl.pallas_call(
            _store,
            out_shape=(jax.ShapeDtypeStruct((k, depth), f32), jax.ShapeDtypeStruct((k, samples), f32)),
            in_specs=[anywhere, anywhere],
            out_specs=(hbm, hbm),
            scratch_shapes=[pltpu.SemaphoreType.DMA((9,))],
            compiler_params=pltpu.CompilerParams(vmem_limit_bytes=1024 * 1024),
        )(w_t, r_t)
        return w_t.T, r_t.T

    return jax.shard_map(
        local_solve,
        mesh=mesh,
        in_specs=(P('prob', 'feat'), P('prob', None), P(('prob', 'feat'), None), P(('prob', 'feat'))),
        out_specs=(P(('prob', 'feat'), None), P('prob', None)),
        check_vma=False,
    )
```

time: 628 us -> 625 us (level)
  no operation moved by 1% of the time
where the time goes in v3:
time: 625 us
  Pallas kernels  624 us (100%)
    pallas_call x1, Pallas kernels, local_solve(): pl.pallas_call(functools.partial(_solve, k, half, top), out_shape=(jax.Sh...  619 us

profile of v3, /device:TPU:113, one launch (start us, length us, event | category | flops | bytes accessed | tf_op | source)
XLA Modules:
  0.0 624.5 jit_solution(7946677236880257808)
XLA Ops:
  0.6 618.6 %shard_map.59 = (f32[200,2048]{1,0:T(8,128)S(1)}, f32[200,16384]{1,0:T(8,128)S(1)}) custom-call(bf16[16384,2048]{1,0:T(8,128)(2,1)} %x_hbm.1, f32[200,16384]{1,0:T(8,128)} %bitcast.5, f32[200,2048]{1,0:T(8,128)} %bitcast.6, f32[1,2048]{1,0:T(1,128)} %bitcast.7), custom_call_target="tpu_custom_call" | custom-call | tf_op jit(solution)/shard_map/pallas_call | solution.py:322
  619.2 5.3 shard_map.60

commit v4 on v3

--- a/solution.py
+++ b/solution.py
@@ -29,7 +29,7 @@
 
 
 def _solve(targets_k, half, top, x_hbm, y_hbm, w_hbm, eta_hbm, w_out, r_out,
-           xbuf, contrib, pair_in, one_r, one_l, two_r, two_l, own, in1_r, in1_l, in2_r, in2_l,
+           xbuf, turned, contrib, pair_in, one_r, one_l, two_r, two_l, own, in1_r, in1_l, in2_r, in2_l,
            shard, gathered, weights, update, gradient, eta,
            x_sem, y_sem, w_sem, out_sem, send_sem, recv_sem):
     samples = x_hbm.shape[0]
@@ -249,14 +249,21 @@
         x_copy(c, buf).wait()
 
         x = xbuf.at[buf]
-        product = lax.dot_general(update[odd], x[...], (((1,), (1,)), ((), ())), preferred_element_type=jnp.float32)
-        for p in range(RING * CORES):
-            contrib[c, p // RING, p % RING] = product[:, p * lanes:(p + 1) * lanes]
+        cut = rows if with_gradient else rows // 2
+        if cut < rows:
+            product = lax.dot_general(
+                update[odd], x[pl.ds(cut, rows - cut)], (((1,), (1,)), ((), ())), preferred_element_type=jnp.float32)
+            for p in range(cut // lanes, RING * CORES):
+                contrib[c, p // RING, p % RING] = product[:, p * lanes - cut:(p + 1) * lanes - cut]
+        turned[:, pl.ds(0, cut)] = x[pl.ds(0, cut)].T
         if with_gradient:
             residual = jnp.concatenate(
                 [gathered[c, p // RING, p % RING] for p in range(RING * CORES)], axis=1)
             term = jnp.dot(residual, x[...], preferred_element_type=jnp.float32)
             gradient[...] = jnp.where(c == 0, 0.0, gradient[...]) + term
+        product = jnp.dot(update[odd], turned[:, pl.ds(0, cut)], preferred_element_type=jnp.float32)
+        for p in range(cut // lanes):
+            contrib[c, p // RING, p % RING] = product[:, p * lanes:(p + 1) * lanes]
         reduce(step)
 
     def run(phase, odd, with_gradient, more):
@@ -326,6 +333,7 @@
             out_specs=(anywhere, anywhere),
             scratch_shapes=[
                 pltpu.VMEM((2, rows, depth), bf16),
+                pltpu.VMEM((depth, rows), bf16),
                 pltpu.VMEM((UNITS, CORES, RING, half, lanes), f32),
                 pltpu.VMEM((UNITS, RING, half, lanes), f32),
                 pltpu.VMEM((UNITS, half, lanes), f32),
@@ -351,7 +359,7 @@
                 pltpu.SemaphoreType.DMA((10, DEPTH)),
             ],
             compiler_params=pltpu.CompilerParams(
-                collective_id=0, has_side_effects=True, vmem_limit_bytes=36 * 1024 * 1024),
+                collective_id=0, has_side_effects=True, vmem_limit_bytes=39 * 1024 * 1024),
         )(design, targets.T, pltpu.with_memory_space_constraint(weights.T, pltpu.HBM),
           pltpu.with_memory_space_constraint(step_sizes[None, :], pltpu.HBM))
         w_t, r_t = pl.pallas_call(

time: 625 us -> 609 us (0.974)
  Pallas kernels: 624 us -> 608 us
    pallas_call x1, Pallas kernels: 619 us -> 603 us  [local_solve(): pl.pallas_call(functools.partial(_solve, k, half, top), out_shape=(jax.Sh...]
where the time goes in v4:
time: 609 us
  Pallas kernels  608 us (100%)
    pallas_call x1, Pallas kernels, local_solve(): pl.pallas_call(functools.partial(_solve, k, half, top), out_shape=(jax.Sh...  603 us

profile of v4, /device:TPU:113, one launch (start us, length us, event | category | flops | bytes accessed | tf_op | source)
XLA Modules:
  0.0 609.0 jit_solution(11475132004288769600)
XLA Ops:
  0.6 603.1 %shard_map.59 = (f32[200,2048]{1,0:T(8,128)S(1)}, f32[200,16384]{1,0:T(8,128)S(1)}) custom-call(bf16[16384,2048]{1,0:T(8,128)(2,1)} %x_hbm.1, f32[200,16384]{1,0:T(8,128)} %bitcast.5, f32[200,2048]{1,0:T(8,128)} %bitcast.6, f32[1,2048]{1,0:T(1,128)} %bitcast.7), custom_call_target="tpu_custom_call" | custom-call | tf_op jit(solution)/shard_map/pallas_call | solution.py:329
  603.7 5.3 shard_map.60
